TPU v7x, 32 devices: a whole 2x2x4 slice. The times are simulated.
32 devices in a mesh: io: 4 (over y, core), comp: 8 (over z, x).
Axes of the slice: x: 2, y: 2, z: 4, core: 2. Of those that a mesh axis runs over, the one named last changes fastest.
Arguments:
- fields: float32 [98304, 256], P(('io', 'comp')), may hold values from -6 to 6
- file_offset: int32 [768, 128], P(('io', 'comp')), may hold values from 0 to 98303, as said below
- level_remap: float32 [4, 64, 64], replicated, may hold values from -0.75 to 0.75
Outputs:
- history: float32 [98304, 256], P(('io', 'comp'))
Inputs may be any that keep to these rules, and one draw needn't show every extreme that they name: file_offset is a permutation of the 98304 file positions. The owner of a position p is the device of flat index p // 3072 (io index times the comp size plus comp index). A device's columns have as owners only itself, devices of its io index and devices of its comp index. To each other device of its io index it sends exactly 8 columns, except the two of comp index one above and one below (cyclically), which get 8 plus between 96 and 192; likewise along io with the devices of its comp index. Two neighbours exchange equally many columns each way, and the count 8 + 192 is reached in every draw. Which columns and positions is drawn.
All inputs are finite; a program needn't handle non-finite values.
Results may differ from a plain program's by a relative error of at most 0.00005.
Values sent between devices are 32-bit elements; how exact they have to be, the bound alone decides.
A program may use at most 64 MiB of HBM per device.

v0:
```python
import jax
import jax.numpy as jnp
from jax import lax
from jax.sharding import PartitionSpec as P

SPREAD = 8
MOST = 192


def remap_levels(values, level_remap):
    field_count = level_remap.shape[0]
    levels = level_remap.shape[1]
    shaped = values.reshape(values.shape[0], field_count, levels)
    mixed = jnp.einsum("cfl,flm->cfm", shaped, level_remap, precision=lax.Precision.HIGHEST)
    return mixed.reshape(values.shape[0], field_count * levels)


def rank_within(target, active, count):
    length = target.shape[0]
    blocks = length // 128
    onehot = (
        (target[:, None] == jnp.arange(count, dtype=jnp.int32)[None, :]) & active[:, None]
    ).astype(jnp.float32)
    blocked = onehot.reshape(blocks, 128, count)
    lower = (jnp.arange(128)[:, None] > jnp.arange(128)[None, :]).astype(jnp.float32)
    inside = jnp.einsum("rs,bsk->brk", lower, blocked, precision=lax.Precision.HIGHEST)
    totals = jnp.sum(blocked, axis=1)
    earlier = (jnp.arange(blocks)[:, None] > jnp.arange(blocks)[None, :]).astype(jnp.float32)
    before = jnp.dot(earlier, totals, precision=lax.Precision.HIGHEST)
    counted = jnp.sum((inside + before[:, None, :]) * blocked, axis=2)
    return counted.reshape(length).astype(jnp.int32)


def pack_slots(values, offsets, slot_index, valid, slots):
    columns = values.shape[0]
    target = jnp.where(valid, slot_index, slots)
    source = (
        jnp.full((slots,), columns, jnp.int32)
        .at[target]
        .set(jnp.arange(columns, dtype=jnp.int32), mode="drop")
    )
    packed = jnp.take(values, source, axis=0, mode="fill", fill_value=0.0)
    packed_offsets = jnp.take(offsets, source, axis=0, mode="fill", fill_value=-1)
    return (packed, packed_offsets)


def per_device(fields, file_offset, level_remap):
    columns, width = fields.shape
    n_io = lax.axis_size("io")
    n_comp = lax.axis_size("comp")
    offsets = file_offset.reshape(columns)
    values = remap_levels(fields, level_remap)
    owner = offsets // columns
    my_group = lax.axis_index("io")
    my_task = lax.axis_index("comp")
    owner_group = owner // n_comp
    owner_task = owner % n_comp
    along_comp = (owner_group == my_group) & (owner_task != my_task)
    along_io = (owner_task == my_task) & (owner_group != my_group)
    stays = (owner_group == my_group) & (owner_task == my_task)
    comp_rank = rank_within(owner_task, along_comp, n_comp)
    io_rank = rank_within(owner_group, along_io, n_io)
    received = []
    capacity = SPREAD + MOST
    comp_rows, comp_offsets = pack_slots(
        values, offsets, owner_task * capacity + comp_rank, along_comp, n_comp * capacity
    )
    got_rows, got_offsets = (
        lax.all_to_all(
            comp_rows.reshape(n_comp, capacity, width),
            "comp",
            split_axis=0,
            concat_axis=0,
            tiled=True,
        ),
        lax.all_to_all(
            comp_offsets.reshape(n_comp, capacity), "comp", split_axis=0, concat_axis=0, tiled=True
        ),
    )
    received.append(
        (got_rows.reshape(n_comp * capacity, width), got_offsets.reshape(n_comp * capacity))
    )
    io_rows, io_offsets = pack_slots(
        values, offsets, owner_group * capacity + io_rank, along_io, n_io * capacity
    )
    got_rows, got_offsets = (
        lax.all_to_all(
            io_rows.reshape(n_io, capacity, width), "io", split_axis=0, concat_axis=0, tiled=True
        ),
        lax.all_to_all(
            io_offsets.reshape(n_io, capacity), "io", split_axis=0, concat_axis=0, tiled=True
        ),
    )
    received.append(
        (got_rows.reshape(n_io * capacity, width), got_offsets.reshape(n_io * capacity))
    )
    local_target = jnp.where(stays, offsets % columns, columns)
    all_rows = jnp.concatenate([values] + [pair[0] for pair in received], axis=0)
    all_targets = jnp.concatenate(
        [local_target]
        + [
            jnp.where(pair[1] >= 0, pair[1] % columns, columns).astype(jnp.int32)
            for pair in received
        ],
        axis=0,
    )
    total_rows = all_rows.shape[0]
    source = (
        jnp.zeros((columns,), jnp.int32)
        .at[all_targets]
        .set(jnp.arange(total_rows, dtype=jnp.int32), mode="drop")
    )
    placed = jnp.take(all_rows, source, axis=0)
    return placed


def solution(mesh):
    placed = (P(("io", "comp"), None), P(("io", "comp"), None), P())
    return jax.shard_map(
        per_device, mesh=mesh, in_specs=placed, out_specs=P(("io", "comp"), None), check_vma=False
    )
```

profile of v0, /device:TPU:0, one launch (start us, length us, event | category | flops | bytes accessed | tf_op | source)
XLA Modules:
  0.0 149.7 jit_solution(8229320943649889707)
XLA Ops:
  0.0 0.8 broadcast_divide_fusion
  0.8 0.7 compare_and_fusion.2
  2.6 11.8 %scatter_custom_fusion.1 = s32[800]{0:T(1024)S(1)} fusion(s32[3072]{0:T(1024)S(1)} %bitcast.59, s32[3072]{0:T(1024)S(1)} %iota.52, s32[]{:T(128)} %constant.130.clone.1), kind=kCustom, calls=%fused_computation.100 | custom fusion | bytes 3204 | tf_op jit(solution)/shard_map/scatter | solution.py:40
  14.4 4.9 %gather_fusion.1 = s32[800]{0:T(1024)S(1)} fusion(s32[3072]{0:T(1024)S(1)} %bitcast.47, s32[1024]{0:T(1024)S(1)} %pad_clamp_fusion.1), kind=kCustom, calls=%fused_computation.1 | custom fusion | bytes 9600 | tf_op jit(solution)/shard_map/jit(_take)/gather | solution.py:43
  20.0 4.3 %all-to-all-start.1 = ((s32[4,1,200]{2,1,0:T(1,128)}), s32[4,1,200]{2,1,0:T(1,128)S(1)}, u32[]{:S(2)}, u32[]{:S(2)}) async-start(s32[4,1,200]{2,1,0:T(1,128)} %select_n.360), calls=%async_computation.1 | async-start | bytes 8192 | tf_op jit(solution)/shard_map/all_to_all | solution.py:90
  24.3 11.8 %scatter_custom_fusion = s32[1600]{0:T(1024)S(1)} fusion(s32[3072]{0:T(1024)S(1)} %bitcast.57, s32[3072]{0:T(1024)S(1)} %iota.51, s32[]{:T(128)} %constant.130.clone.1), kind=kCustom, calls=%fused_computation.96 | custom fusion | bytes 6404 | tf_op jit(solution)/shard_map/scatter | solution.py:40
  36.1 8.8 %gather_fusion = s32[1600]{0:T(1024)S(1)} fusion(s32[3072]{0:T(1024)S(1)} %bitcast.48, s32[2048]{0:T(1024)S(1)} %pad_clamp_fusion), kind=kCustom, calls=%fused_computation | custom fusion | bytes 19200 | tf_op jit(solution)/shard_map/jit(_take)/gather | solution.py:43
  44.9 2.4 %copy.17 = f32[3072,256]{0,1:T(8,128)S(1)} copy(f32[3072,256]{1,0:T(8,128)} %param.3) | data formatting | bytes 6291456 | tf_op args[0]
  47.3 4.5 %fusion.38 = f32[4,64,3072]{2,1,0:T(8,128)} fusion(f32[4,64,64]{2,1,0:T(8,128)S(1)} %copy-done, f32[3072,4,64]{0,2,1:T(8,128)S(1)} %bitcast.50), kind=kOutput, calls=%fused_computation.102 | convolution fusion | flops 603979776 | bytes 6356992 | tf_op jit(solution)/shard_map/cfl,flm->cfm/dot_general | solution.py:14
  51.8 2.4 %copy.21 = f32[3072,256]{1,0:T(8,128)S(1)} copy(f32[3072,256]{0,1:T(8,128)} %bitcast.49) | data formatting | bytes 6291456 | tf_op jit(solution)/shard_map/reshape | solution.py:15
  54.2 3.4 %gather_fusion.3 = f32[800,256]{1,0:T(8,128)} fusion(f32[3072,256]{1,0:T(8,128)S(1)} %copy.21, s32[1024]{0:T(1024)S(1)} %pad_clamp_fusion.1), kind=kCustom, calls=%fused_computation.3 | custom fusion | bytes 1641600 | tf_op jit(solution)/shard_map/jit(_take)/gather | solution.py:42
  58.4 6.3 %all-to-all-start = ((s32[8,1,200]{2,1,0:T(1,128)}), s32[8,1,200]{2,1,0:T(1,128)S(1)}, u32[]{:S(2)}, u32[]{:S(2)}) async-start(s32[8,1,200]{2,1,0:T(1,128)} %select_n.353), calls=%async_computation | async-start | bytes 16384 | tf_op jit(solution)/shard_map/all_to_all | solution.py:76
  64.6 2.2 %broadcast_select_fusion.2 = f32[4,200,256]{2,1,0:T(8,128)} fusion(f32[4,200,256]{2,1,0:T(8,128)} %bitcast.52, pred[4,200]{1,0:T(4,128)(4,1)S(1)} %broadcast_in_dim.107), kind=kLoop, calls=%fused_computation.19 | loop fusion | flops 204800 | bytes 1639200 | tf_op jit(solution)/shard_map/jit(_take)/select_n | solution.py:42
  66.8 4.3 %all-to-all-done = s32[8,1,200]{2,1,0:T(1,128)S(1)} async-done(((s32[8,1,200]{2,1,0:T(1,128)}), s32[8,1,200]{2,1,0:T(1,128)S(1)}, u32[]{:S(2)}, u32[]{:S(2)}) %all-to-all-start) | async-done | bytes 6432 | tf_op jit(solution)/shard_map/all_to_all | solution.py:76
  71.2 4.2 %all-to-all-start.3 = ((f32[4,200,256]{2,1,0:T(8,128)}), f32[4,200,256]{2,1,0:T(8,128)}, u32[]{:S(2)}, u32[]{:S(2)}) async-start(f32[4,200,256]{2,1,0:T(8,128)} %broadcast_select_fusion.2), calls=%async_computation.3 | async-start | bytes 1638400 | tf_op jit(solution)/shard_map/all_to_all | solution.py:87
  75.4 5.2 %gather_fusion.2 = f32[1600,256]{1,0:T(8,128)} fusion(f32[3072,256]{1,0:T(8,128)S(1)} %copy.21, s32[2048]{0:T(1024)S(1)} %pad_clamp_fusion), kind=kCustom, calls=%fused_computation.2 | custom fusion | bytes 3283200 | tf_op jit(solution)/shard_map/jit(_take)/gather | solution.py:42
  80.7 2.9 %broadcast_select_fusion.1 = f32[8,200,256]{2,1,0:T(8,128)} fusion(f32[8,200,256]{2,1,0:T(8,128)} %bitcast.51, pred[8,200]{1,0:T(8,128)(4,1)S(1)} %broadcast_in_dim.104), kind=kLoop, calls=%fused_computation.18 | loop fusion | flops 409600 | bytes 3278400 | tf_op jit(solution)/shard_map/jit(_take)/select_n | solution.py:42
  83.6 3.8 %all-to-all-done.3 = f32[4,200,256]{2,1,0:T(8,128)} async-done(((f32[4,200,256]{2,1,0:T(8,128)}), f32[4,200,256]{2,1,0:T(8,128)}, u32[]{:S(2)}, u32[]{:S(2)}) %all-to-all-start.3) | async-done | bytes 819232 | tf_op jit(solution)/shard_map/all_to_all | solution.py:87
  87.4 4.3 %all-to-all-start.2 = ((f32[8,200,256]{2,1,0:T(8,128)}), f32[8,200,256]{2,1,0:T(8,128)}, u32[]{:S(2)}, u32[]{:S(2)}) async-start(f32[8,200,256]{2,1,0:T(8,128)} %broadcast_select_fusion.1), calls=%async_computation.2 | async-start | bytes 3276800 | tf_op jit(solution)/shard_map/all_to_all | solution.py:69
  92.5 26.4 %scatter_custom_fusion.2 = s32[3072]{0:T(1024)S(1)} fusion(s32[5472]{0:T(1024)S(1)} %fusion.17, s32[5472]{0:T(1024)S(1)} %iota.53, s32[]{:T(128)} %constant.128.clone.1), kind=kCustom, calls=%fused_computation.90 | custom fusion | bytes 12292 | tf_op jit(solution)/shard_map/scatter | solution.py:111
  119.0 11.1 %all-to-all-done.2 = f32[8,200,256]{2,1,0:T(8,128)} async-done(((f32[8,200,256]{2,1,0:T(8,128)}), f32[8,200,256]{2,1,0:T(8,128)}, u32[]{:S(2)}, u32[]{:S(2)}) %all-to-all-start.2) | async-done | bytes 1638432 | tf_op jit(solution)/shard_map/all_to_all | solution.py:69
  130.1 4.5 %pad_maximum_fusion = f32[5472,256]{1,0:T(8,128)} fusion(f32[800,256]{1,0:T(8,128)} %bitcast.17, f32[1600,256]{1,0:T(8,128)} %bitcast.15, f32[3072,256]{1,0:T(8,128)S(1)} %copy.21), kind=kLoop, calls=%fused_computation.8 | loop fusion | flops 2801664 | bytes 11206656 | tf_op jit(solution)/shard_map/concatenate | solution.py:98
  134.6 12.4 %gather_fusion.4 = f32[3072,256]{1,0:T(8,128)S(1)} fusion(f32[5472,256]{1,0:T(8,128)} %pad_maximum_fusion, s32[3072]{0:T(1024)S(1)} %fusion.28), kind=kCustom, calls=%fused_computation.4 | custom fusion | bytes 6303744 | tf_op jit(solution)/shard_map/jit(_take)/gather | solution.py:113
  147.0 2.7 %broadcast_select_fusion = f32[3072,256]{1,0:T(8,128)} fusion(f32[3072,256]{1,0:T(8,128)S(1)} %gather_fusion.4, pred[3072]{0:T(1024)(128)(4,1)S(1)} %compare_and_fusion), kind=kLoop, calls=%fused_computation.9 | loop fusion | flops 786432 | bytes 6294528 | tf_op jit(solution)/shard_map/jit(_take)/select_n | solution.py:113
  (46 shorter events, 3.4 us)
Async XLA Ops:
  0.0 47.3 %copy-start = (f32[4,64,64]{2,1,0:T(8,128)S(1)}, f32[4,64,64]{2,1,0:T(8,128)}, u32[]{:S(2)}) copy-start(f32[4,64,64]{2,1,0:T(8,128)} %param.5) | copy-start | bytes 196612
  0.0 14.4 %copy-start.1 = (s32[24,128]{1,0:T(8,128)S(1)}, s32[24,128]{1,0:T(8,128)}, u32[]{:S(2)}) copy-start(s32[24,128]{1,0:T(8,128)} %param.4) | copy-start | bytes 36868
  20.0 38.3 %all-to-all-start.1 = ((s32[4,1,200]{2,1,0:T(1,128)}), s32[4,1,200]{2,1,0:T(1,128)S(1)}, u32[]{:S(2)}, u32[]{:S(2)}) async-start(s32[4,1,200]{2,1,0:T(1,128)} %select_n.360), calls=%async_computation.1 | async-start | bytes 8192 | tf_op jit(solution)/shard_map/all_to_all | solution.py:90
  58.4 12.8 %all-to-all-start = ((s32[8,1,200]{2,1,0:T(1,128)}), s32[8,1,200]{2,1,0:T(1,128)S(1)}, u32[]{:S(2)}, u32[]{:S(2)}) async-start(s32[8,1,200]{2,1,0:T(1,128)} %select_n.353), calls=%async_computation | async-start | bytes 16384 | tf_op jit(solution)/shard_map/all_to_all | solution.py:76
  71.2 16.3 %all-to-all-start.3 = ((f32[4,200,256]{2,1,0:T(8,128)}), f32[4,200,256]{2,1,0:T(8,128)}, u32[]{:S(2)}, u32[]{:S(2)}) async-start(f32[4,200,256]{2,1,0:T(8,128)} %broadcast_select_fusion.2), calls=%async_computation.3 | async-start | bytes 1638400 | tf_op jit(solution)/shard_map/all_to_all | solution.py:87
  87.4 42.7 %all-to-all-start.2 = ((f32[8,200,256]{2,1,0:T(8,128)}), f32[8,200,256]{2,1,0:T(8,128)}, u32[]{:S(2)}, u32[]{:S(2)}) async-start(f32[8,200,256]{2,1,0:T(8,128)} %broadcast_select_fusion.1), calls=%async_computation.2 | async-start | bytes 3276800 | tf_op jit(solution)/shard_map/all_to_all | solution.py:69
where the time goes:
time: 150 us
  local copies, waits for them, and re-layouts  91.4 us (61%)
  waiting for transfers between devices  19.3 us (13%)
  starting transfers between devices  19.1 us (13%)
  other arithmetic  14.5 us (10%)
  matrix products  5.16 us (3%)
    scatter x1, local copies, waits for them, and re-layouts, per_device(): source = jnp.zeros((columns,), jnp.int32).at[all_targets].set(jnp.arange(...  26.4 us
    scatter x2, local copies, waits for them, and re-layouts, pack_slots(): source = jnp.full((slots,), columns, jnp.int32).at[target].set(jnp.arange...  23.6 us
    gather x2, local copies, waits for them, and re-layouts, pack_slots(): jnp.take(offsets, source, axis=0, mode='fill', fill_value=-1)  13.7 us
    gather x1, local copies, waits for them, and re-layouts, per_device(): placed = jnp.take(all_rows, source, axis=0)  12.4 us
    all_to_all x1, waiting for transfers between devices, per_device(): lax.all_to_all(comp_rows.reshape(n_comp, capacity, width), 'comp', split_...  11.1 us
    gather x2, local copies, waits for them, and re-layouts, pack_slots(): packed = jnp.take(values, source, axis=0, mode='fill', fill_value=0.0)  8.6 us
    all_to_all x1, starting transfers between devices, per_device(): lax.all_to_all(comp_offsets.reshape(n_comp, capacity), 'comp', split_axis...  6.28 us
    select_n x2, other arithmetic, pack_slots(): packed = jnp.take(values, source, axis=0, mode='fill', fill_value=0.0)  5.08 us
  transfers between devices with their start and end apart: 4, of which 3 were waited for; matrix products, arithmetic and copies ran while one was open for 48% of the time, Pallas kernels for 0%

commit v1 on v0

v1 whole, which is shorter than its diff:
```python
import functools

import jax
import jax.numpy as jnp
from jax import lax
from jax.experimental import pallas as pl
from jax.experimental.pallas import tpu as pltpu
from jax.sharding import PartitionSpec as P

SPREAD = 8
MOST = 192
NEAR = SPREAD + MOST
NEAR_ROWS = -(-NEAR // 128)
LIMIT = 24 * 1024 * 1024
I32 = jnp.int32
F32 = jnp.float32
BF16 = jnp.bfloat16


def whole_part(value, divisor):
    return ((value.astype(F32) + 0.5) * (1.0 / divisor)).astype(I32)


def view_row(row):
    return ((row >> 3) << 4) + (row & 7)


def route_kernel(n_io, n_comp, off_ref, src_ref, near_ref, far_ref):
    rows = off_ref.shape[0]
    columns = rows * 128
    far = far_ref.shape[0]
    kinds = 4 + far
    my_group = lax.axis_index("io")
    my_task = lax.axis_index("comp")
    offset = off_ref[...]
    owner = whole_part(offset, columns)
    place = offset - owner * columns
    group = whole_part(owner, n_comp)
    task = owner - group * n_comp
    step_c = task - my_task
    step_c = jnp.where(step_c < 0, step_c + n_comp, step_c)
    step_g = group - my_group
    step_g = jnp.where(step_g < 0, step_g + n_io, step_g)
    kind_c = jnp.where(step_c == 1, 0, jnp.where(step_c == n_comp - 1, 1, step_c + 2))
    kind_g = jnp.where(
        step_g == 1, 2, jnp.where(step_g == n_io - 1, 3, step_g + (2 + n_comp - 3))
    )
    stays = (step_c == 0) & (step_g == 0)
    kind = jnp.where(stays, -1, jnp.where(step_g == 0, kind_c, kind_g))

    masks = [(kind == k).astype(F32) for k in range(kinds)]
    stacked = jnp.concatenate(masks, axis=0).astype(BF16)
    r2 = lax.broadcasted_iota(I32, (128, 256), 0)
    c2 = lax.broadcasted_iota(I32, (128, 256), 1)
    tri = ((c2 >= 128) | (r2 < c2)).astype(F32).astype(BF16)
    both = jnp.dot(stacked, tri, preferred_element_type=F32)
    totals = jnp.concatenate(
        [both[k * rows : (k + 1) * rows, 128:] for k in range(kinds)], axis=1
    ).astype(BF16)
    lr = lax.broadcasted_iota(I32, (rows, rows), 0)
    lc = lax.broadcasted_iota(I32, (rows, rows), 1)
    lower = (lr > lc).astype(F32).astype(BF16)
    before = jnp.dot(lower, totals, preferred_element_type=F32)
    rank = jnp.zeros((rows, 128), F32)
    for k in range(kinds):
        rank += masks[k] * (
            both[k * rows : (k + 1) * rows, :128] + before[:, k * 128 : (k + 1) * 128]
        )
    rank = rank.astype(I32)

    base = jnp.where(kind < 4, rows + NEAR_ROWS * kind, rows + (NEAR_ROWS - 1) * 4 + kind)
    high = jnp.where(stays, place >> 7, base + (rank >> 7))
    low = jnp.where(stays, place & 127, rank & 127)
    place_high = (place >> 7).astype(F32) + 1.0
    place_low = (place & 127).astype(F32)

    total = src_ref.shape[0]
    hi_iota = lax.broadcasted_iota(I32, (total, 128), 0)
    lane_iota = lax.broadcasted_iota(I32, (total, 128), 1).astype(F32)
    lo_iota = lax.broadcasted_iota(I32, (128, 128), 0)
    acc = jnp.zeros((4 * total, 128), F32)
    for r in range(rows):
        hit = (hi_iota == high[r : r + 1, :]).astype(F32)
        left = jnp.concatenate(
            [
                hit * float(r),
                hit * lane_iota,
                hit * place_high[r : r + 1, :],
                hit * place_low[r : r + 1, :],
            ],
            axis=0,
        ).astype(BF16)
        right = (lo_iota == low[r : r + 1, :]).astype(F32).astype(BF16)
        acc += lax.dot_general(
            left, right, (((1,), (1,)), ((), ())), preferred_element_type=F32
        )
    found = acc.astype(I32)
    src_ref[...] = view_row(found[:total] * 128 + found[total : 2 * total])
    p_high = found[2 * total : 3 * total]
    target = (p_high - 1) * 128 + found[3 * total :]
    target = jnp.where(p_high > 0, view_row(target), 2 * columns)
    for k in range(4):
        near_ref[k] = target[rows + NEAR_ROWS * k : rows + NEAR_ROWS * (k + 1)]
    for j in range(far):
        at = rows + NEAR_ROWS * 4 + j
        far_ref[j] = target[at : at + 1]


def partners(n_io, n_comp):
    near = [("comp", 1), ("comp", n_comp - 1), ("io", 1), ("io", n_io - 1)]
    far = [("comp", d) for d in range(2, n_comp - 1)] + [("io", d) for d in range(2, n_io - 1)]
    return near, far


def mix(rows, weights):
    m = rows.shape[0] // 16
    parts = rows.reshape(m, 2, 8, 128)
    outs = []
    for h in range(2):
        x = parts[:, h].reshape(8 * m, 128)
        head = x.astype(BF16)
        tail = (x - head.astype(F32)).astype(BF16)
        y = jnp.dot(
            jnp.concatenate([head, tail], axis=1), weights[h], preferred_element_type=F32
        )
        outs.append((y[:, :128] + y[:, 128:]).reshape(m, 1, 8, 128))
    return jnp.concatenate(outs, axis=1).reshape(16 * m, 128)


def exchange_kernel(
    n_io,
    n_comp,
    src_ref,
    near_ref,
    far_ref,
    fields_ref,
    map_ref,
    block_ref,
    got_ref,
    near_out,
    far_out,
    send,
    recv,
    near_in,
    far_in,
    wide,
    row_send,
    row_recv,
    pos_send,
    pos_recv,
):
    view = fields_ref.shape[0]
    columns = view // 2
    near, far = partners(n_io, n_comp)
    sizes = {"io": n_io, "comp": n_comp}
    where = {"io": lax.axis_index("io"), "comp": lax.axis_index("comp")}

    def device(axis, step):
        return {axis: lax.rem(where[axis] + step, sizes[axis])}

    everyone = near + far
    barrier = pltpu.get_barrier_semaphore()
    for axis, step in everyone:
        pl.semaphore_signal(
            barrier, inc=1, device_id=device(axis, step), device_id_type=pl.DeviceIdType.MESH
        )

    def fetch(count, source, target, target_ref):
        def body(i, carry):
            got = [
                fields_ref[pl.ds(src_ref[source + i * 8 + s], 2, stride=8), :] for s in range(8)
            ]
            for s in range(8):
                target_ref[pl.ds(target + i * 16 + s, 2, stride=8), :] = got[s]
            return carry

        lax.fori_loop(0, count // 8, body, 0)

    copies = []

    def ship(source, target, sem_at, axis, step, sends, recvs):
        copy = pltpu.make_async_remote_copy(
            src_ref=source,
            dst_ref=target,
            send_sem=sends.at[sem_at],
            recv_sem=recvs.at[sem_at],
            device_id=device(axis, step),
            device_id_type=pl.DeviceIdType.MESH,
        )
        copy.start()
        copies.append(copy)

    for k in range(4):
        fetch(NEAR, columns + k * NEAR_ROWS * 128, k * 2 * NEAR, send)
        if k == 0:
            pl.semaphore_wait(barrier, len(everyone))
        axis, step = near[k]
        part = pl.ds(k * 2 * NEAR, 2 * NEAR)
        ship(send.at[part], recv.at[part], k, axis, step, row_send, row_recv)
    for j, (axis, step) in enumerate(far):
        start = 8 * NEAR + 16 * j
        fetch(8, columns + (4 * NEAR_ROWS + j) * 128, start, send)
        part = pl.ds(start, 16)
        ship(send.at[part], recv.at[part], 4 + j, axis, step, row_send, row_recv)
    for k, (axis, step) in enumerate(near):
        ship(near_ref.at[k], near_in.at[k], k, axis, step, pos_send, pos_recv)
    for j, (axis, step) in enumerate(far):
        ship(far_ref.at[j], far_in.at[j], 4 + j, axis, step, pos_send, pos_recv)

    weights = []
    for h in range(2):
        wide[...] = jnp.zeros((128, 128), F32)
        wide[:64, :64] = map_ref[2 * h]
        wide[64:, 64:] = map_ref[2 * h + 1]
        full = wide[...]
        head = full.astype(BF16)
        tail = (full - head.astype(F32)).astype(BF16)
        line = jnp.concatenate([head, tail], axis=1)
        weights.append(jnp.concatenate([line, line], axis=0))

    fetch(columns, 0, 0, block_ref)
    chunk = 512

    def mix_block(i, carry):
        at = pl.ds(i * chunk, chunk)
        block_ref[at, :] = mix(block_ref[at, :], weights)
        return carry

    lax.fori_loop(0, view // chunk, mix_block, 0)

    for copy in copies:
        copy.wait()
    for k in range(4):
        part = slice(k * 2 * NEAR, (k + 1) * 2 * NEAR)
        got_ref[part, :] = mix(recv[part, :], weights)
    part = slice(8 * NEAR, send.shape[0])
    got_ref[part, :] = mix(recv[part, :], weights)
    near_out[...] = near_in[...]
    far_out[...] = far_in[...]


def place_kernel(near_ref, far_ref, block_in, got_ref, block_ref, out_ref, sem):
    def put(count, source, index_ref, index):
        def body(i, carry):
            rows = [got_ref[pl.ds(source + i * 16 + s, 2, stride=8), :] for s in range(8)]
            for s in range(8):
                block_ref[pl.ds(index_ref[index + i * 8 + s], 2, stride=8), :] = rows[s]
            return carry

        lax.fori_loop(0, count // 8, body, 0)

    for k in range(4):
        put(NEAR, k * 2 * NEAR, near_ref, k * NEAR_ROWS * 128)
    for j in range(far_ref.shape[0] // 128):
        put(8, 8 * NEAR + 16 * j, far_ref, j * 128)
    copy = pltpu.make_async_copy(block_ref.at[pl.ds(0, out_ref.shape[0])], out_ref, sem)
    copy.start()
    copy.wait()


def per_device(fields, file_offset, level_remap):
    columns, width = fields.shape
    n_io = lax.axis_size("io")
    n_comp = lax.axis_size("comp")
    near, far = partners(n_io, n_comp)
    count = len(far)
    rows = file_offset.shape[0]
    total = -(-(rows + 4 * NEAR_ROWS + count) // 8) * 8
    vmem = pl.BlockSpec(memory_space=pltpu.VMEM)
    smem = pl.BlockSpec(memory_space=pltpu.SMEM)
    hbm = pl.BlockSpec(memory_space=pl.ANY)

    src, near_pos, far_pos = pl.pallas_call(
        functools.partial(route_kernel, n_io, n_comp),
        out_shape=(
            jax.ShapeDtypeStruct((total, 128), I32),
            jax.ShapeDtypeStruct((4, NEAR_ROWS, 128), I32),
            jax.ShapeDtypeStruct((count, 1, 128), I32),
        ),
        in_specs=[vmem],
        out_specs=(vmem,) * 3,
        compiler_params=pltpu.CompilerParams(vmem_limit_bytes=LIMIT),
        name="route",
    )(file_offset)

    view = fields.reshape(columns // 8, 8, 2, 128).transpose(0, 2, 1, 3).reshape(2 * columns, 128)
    slots = 4 * NEAR + 8 * count
    kinds = 4 + count
    block, got, near_got, far_got = pl.pallas_call(
        functools.partial(exchange_kernel, n_io, n_comp),
        out_shape=(
            pltpu.VMEM((2 * columns + 16, 128), F32),
            jax.ShapeDtypeStruct((2 * slots, 128), F32),
            jax.ShapeDtypeStruct((4, NEAR_ROWS, 128), I32),
            jax.ShapeDtypeStruct((count, 1, 128), I32),
        ),
        in_specs=[smem, vmem, vmem, vmem, vmem],
        out_specs=(vmem,) * 4,
        scratch_shapes=[
            pltpu.VMEM((2 * slots, 128), F32),
            pltpu.VMEM((2 * slots, 128), F32),
            pltpu.VMEM((4, NEAR_ROWS, 128), I32),
            pltpu.VMEM((count, 1, 128), I32),
            pltpu.VMEM((128, 128), F32),
            pltpu.SemaphoreType.DMA((kinds,)),
            pltpu.SemaphoreType.DMA((kinds,)),
            pltpu.SemaphoreType.DMA((kinds,)),
            pltpu.SemaphoreType.DMA((kinds,)),
        ],
        compiler_params=pltpu.CompilerParams(
            collective_id=0, has_side_effects=True, vmem_limit_bytes=LIMIT
        ),
        name="exchange",
    )(src.reshape(-1), near_pos, far_pos, view, level_remap)

    _, out = pl.pallas_call(
        place_kernel,
        out_shape=(
            pltpu.VMEM(block.shape, F32),
            jax.ShapeDtypeStruct((2 * columns, 128), F32),
        ),
        in_specs=[smem, smem, vmem, vmem],
        out_specs=(vmem, hbm),
        scratch_shapes=[pltpu.SemaphoreType.DMA],
        input_output_aliases={2: 0},
        compiler_params=pltpu.CompilerParams(vmem_limit_bytes=LIMIT),
        name="place",
    )(near_got.reshape(-1), far_got.reshape(-1), block, got)
    return out.reshape(columns // 8, 2, 8, 128).transpose(0, 2, 1, 3).reshape(columns, width)


def solution(mesh):
    placed = (P(("io", "comp"), None), P(("io", "comp"), None), P())
    return jax.shard_map(
        per_device, mesh=mesh, in_specs=placed, out_specs=P(("io", "comp"), None), check_vma=False
    )
```

time: 150 us -> 28.6 us (0.19)
  local copies, waits for them, and re-layouts: 91.4 us -> 5.56 us
  Pallas kernels: 0 us -> 22.7 us
  waiting for transfers between devices: 19.3 us -> 0 us
  starting transfers between devices: 19.1 us -> 0 us
  other arithmetic: 14.5 us -> 0.01 us
  matrix products: 5.16 us -> 0 us
    scatter x3 -> x0, local copies, waits for them, and re-layouts: 50 us -> none  [the longest x1 26.4 us: per_device(): source = jnp.zeros((columns,), jnp.int32).at[all_targets].set(jnp.arange(...]
    gather x5 -> x0, local copies, waits for them, and re-layouts: 34.7 us -> none  [the longest x2 13.7 us: pack_slots(): jnp.take(offsets, source, axis=0, mode='fill', fill_value=-1)]
    pallas_call x0 -> x3, Pallas kernels: none -> 22.7 us  [the longest x1 18.3 us: per_device(): pl.pallas_call(functools.partial(exchange_kernel, n_io, n_comp), out_shap...]
    all_to_all x4 -> x0, waiting for transfers between devices: 19.3 us -> none  [the longest x1 11.1 us: per_device(): lax.all_to_all(comp_rows.reshape(n_comp, capacity, width), 'comp', split_...]
    all_to_all x4 -> x0, starting transfers between devices: 19.1 us -> none  [the longest x1 6.28 us: per_device(): lax.all_to_all(comp_offsets.reshape(n_comp, capacity), 'comp', split_axis...]
    select_n x13 -> x0, other arithmetic: 8.15 us -> none  [the longest x2 5.08 us: pack_slots(): packed = jnp.take(values, source, axis=0, mode='fill', fill_value=0.0)]
    dot_general x5 -> x0, matrix products: 5.16 us -> none  [the longest x1 4.52 us: remap_levels(): jnp.einsum('cfl,flm->cfm', shaped, level_remap, precision=lax.Precision.H...]
    concatenate x1 -> x0, other arithmetic: 4.47 us -> none  [per_device(): jnp.concatenate([values] + [pair[0] for pair in received], axis=0)]
  transfers between devices with their start and end apart: 4 -> 0, of which waited for: 3 -> 0; matrix products, arithmetic and copies ran while one was open for 48% -> 0% of each run, Pallas kernels for 0% -> 0%
where the time goes in v1:
time: 28.6 us; the launch traced here: 28.3 us
  Pallas kernels  22.7 us (79%)
  local copies, waits for them, and re-layouts  5.56 us (19%)
    pallas_call x1, Pallas kernels, per_device(): pl.pallas_call(functools.partial(exchange_kernel, n_io, n_comp), out_shap...  18.3 us
    unnamed x10, local copies, waits for them, and re-layouts  5.56 us
    pallas_call x1, Pallas kernels, per_device(): pl.pallas_call(place_kernel, out_shape=(pltpu.VMEM(block.shape, F32), jax...  3.48 us
    pallas_call x1, Pallas kernels, per_device(): pl.pallas_call(functools.partial(route_kernel, n_io, n_comp), out_shape=(...  0.99 us

profile of v1, /device:TPU:0, one launch (start us, length us, event | category | flops | bytes accessed | tf_op | source)
XLA Modules:
  0.0 28.3 jit_solution(10506502821955742977)
XLA Ops:
  0.0 0.0 copy-start.4
  0.0 0.7 %copy-done.4 = s32[24,128]{1,0:T(8,128)S(1)} copy-done((s32[24,128]{1,0:T(8,128)S(1)}, s32[24,128]{1,0:T(8,128)}, u32[]{:S(2)}) %copy-start.4) | copy-done | bytes 12312
  0.7 1.0 %route.1 = (s32[40,128]{1,0:T(8,128)S(1)}, s32[4,2,128]{2,1,0:T(2,128)S(1)}, s32[6,1,128]{2,1,0:T(1,128)S(1)}) custom-call(s32[24,128]{1,0:T(8,128)S(1)} %copy-done.4), custom_call_target="tpu_custom_call" | custom-call | tf_op jit(solution)/shard_map/route/pallas_call | solution.py:273
  1.7 0.0 copy-start
  1.7 1.9 %copy-done = f32[3072,256]{1,0:T(8,128)S(1)} copy-done((f32[3072,256]{1,0:T(8,128)S(1)}, f32[3072,256]{1,0:T(8,128)}, u32[]{:S(2)}) %copy-start) | copy-done | bytes 3145752
  3.6 0.0 copy-start.3
  3.6 0.9 %copy-done.3 = f32[4,64,64]{2,1,0:T(8,128)S(1)} copy-done((f32[4,64,64]{2,1,0:T(8,128)S(1)}, f32[4,64,64]{2,1,0:T(8,128)}, u32[]{:S(2)}) %copy-start.3) | copy-done | bytes 65560
  4.5 18.3 %exchange.1 = (f32[6160,128]{1,0:T(8,128)S(1)}, f32[1696,128]{1,0:T(8,128)S(1)}, s32[4,2,128]{2,1,0:T(2,128)S(1)}, s32[6,1,128]{2,1,0:T(1,128)S(1)}) custom-call(s32[5120]{0:T(1024)S(1)} %bitcast.14, s32[4,2,128]{2,1,0:T(2,128)S(1)} %get-tuple-element.14.near_ref, s32[6,1,128]{2,1,0:T(1,128)S(1)} %get-tuple-element.15.far_ref, f32[6144,128]{1,0:T(8,128)S(1)} %bitcast.13, ...), custom_call_target="tpu_custom_call" | custom-call | tf_op jit(solution)/shard_map/exchange/pallas_call | solution.py:289
  22.8 0.0 copy-start.1
  22.8 0.9 %copy-done.1 = f32[1696,128]{1,0:T(8,128)} copy-done((f32[1696,128]{1,0:T(8,128)}, f32[1696,128]{1,0:T(8,128)S(1)}, u32[]{:S(2)}) %copy-start.1) | copy-done | bytes 868376
  23.7 0.0 copy-start.2
  23.7 1.2 %copy-done.2 = f32[1696,128]{1,0:T(8,128)S(1)} copy-done((f32[1696,128]{1,0:T(8,128)S(1)}, f32[1696,128]{1,0:T(8,128)}, u32[]{:S(2)}) %copy-start.2) | copy-done | bytes 868376
  24.9 3.5 %place.1 = (f32[6160,128]{1,0:T(8,128)S(1)}, f32[6144,128]{1,0:T(8,128)}) custom-call(s32[1024]{0:T(1024)S(1)} %bitcast.16, s32[768]{0:T(1024)S(1)} %bitcast.15, f32[6160,128]{1,0:T(8,128)S(1)} %get-tuple-element.18.block_in, f32[1696,128]{1,0:T(8,128)S(1)} %copy-done.2), custom_call_target="tpu_custom_call", output_to_operand_aliasing={{0}: (2, {})} | custom-call | tf_op jit(solution)/shard_map/place/pallas_call | solution.py:316
  (1 shorter events, 0.0 us)
Async XLA Ops:
  0.0 0.7 %copy-start.4 = (s32[24,128]{1,0:T(8,128)S(1)}, s32[24,128]{1,0:T(8,128)}, u32[]{:S(2)}) copy-start(s32[24,128]{1,0:T(8,128)} %off_ref.1) | copy-start | bytes 36868
  1.7 1.9 %copy-start = (f32[3072,256]{1,0:T(8,128)S(1)}, f32[3072,256]{1,0:T(8,128)}, u32[]{:S(2)}) copy-start(f32[3072,256]{1,0:T(8,128)} %param.3) | copy-start | bytes 9437188
  3.6 0.9 %copy-start.3 = (f32[4,64,64]{2,1,0:T(8,128)S(1)}, f32[4,64,64]{2,1,0:T(8,128)}, u32[]{:S(2)}) copy-start(f32[4,64,64]{2,1,0:T(8,128)} %map_ref.1) | copy-start | bytes 196612
  22.8 0.9 %copy-start.1 = (f32[1696,128]{1,0:T(8,128)}, f32[1696,128]{1,0:T(8,128)S(1)}, u32[]{:S(2)}) copy-start(f32[1696,128]{1,0:T(8,128)S(1)} %get-tuple-element.19.got_ref) | copy-start | bytes 2605060
  23.7 1.2 %copy-start.2 = (f32[1696,128]{1,0:T(8,128)S(1)}, f32[1696,128]{1,0:T(8,128)}, u32[]{:S(2)}) copy-start(f32[1696,128]{1,0:T(8,128)} %copy-done.1) | copy-start | bytes 2605060

commit v2 on v1

--- a/solution.py
+++ b/solution.py
@@ -11,6 +11,7 @@
 MOST = 192
 NEAR = SPREAD + MOST
 NEAR_ROWS = -(-NEAR // 128)
+PIECES = 4
 LIMIT = 24 * 1024 * 1024
 I32 = jnp.int32
 F32 = jnp.float32
@@ -25,8 +26,39 @@
     return ((row >> 3) << 4) + (row & 7)
 
 
-def route_kernel(n_io, n_comp, off_ref, src_ref, near_ref, far_ref):
+def route_kernel(
+    n_io,
+    n_comp,
+    off_hbm,
+    fields_hbm,
+    map_hbm,
+    src_ref,
+    near_ref,
+    far_ref,
+    fields_ref,
+    weight_ref,
+    off_ref,
+    map_ref,
+    wide,
+    sems,
+):
     rows = off_ref.shape[0]
+    off_copy = pltpu.make_async_copy(off_hbm, off_ref, sems.at[PIECES])
+    off_copy.start()
+    piece = fields_ref.shape[0] // PIECES
+    loads = [
+        pltpu.make_async_copy(
+            fields_hbm.at[pl.ds(i * piece, piece)],
+            fields_ref.at[pl.ds(i * piece, piece)],
+            sems.at[i],
+        )
+        for i in range(PIECES)
+    ]
+    for load in loads:
+        load.start()
+    map_copy = pltpu.make_async_copy(map_hbm, map_ref, sems.at[PIECES + 1])
+    map_copy.start()
+    off_copy.wait()
     columns = rows * 128
     far = far_ref.shape[0]
     kinds = 4 + far
@@ -105,6 +137,19 @@
         at = rows + NEAR_ROWS * 4 + j
         far_ref[j] = target[at : at + 1]
 
+    map_copy.wait()
+    for h in range(2):
+        wide[...] = jnp.zeros((128, 128), F32)
+        wide[:64, :64] = map_ref[2 * h]
+        wide[64:, 64:] = map_ref[2 * h + 1]
+        full = wide[...]
+        head = full.astype(BF16)
+        tail = (full - head.astype(F32)).astype(BF16)
+        line = jnp.concatenate([head, tail], axis=1)
+        weight_ref[h] = jnp.concatenate([line, line], axis=0)
+    for load in loads:
+        load.wait()
+
 
 def partners(n_io, n_comp):
     near = [("comp", 1), ("comp", n_comp - 1), ("io", 1), ("io", n_io - 1)]
@@ -134,16 +179,14 @@
     near_ref,
     far_ref,
     fields_ref,
-    map_ref,
+    weight_ref,
     block_ref,
-    got_ref,
     near_out,
     far_out,
     send,
     recv,
     near_in,
     far_in,
-    wide,
     row_send,
     row_recv,
     pos_send,
@@ -207,17 +250,7 @@
     for j, (axis, step) in enumerate(far):
         ship(far_ref.at[j], far_in.at[j], 4 + j, axis, step, pos_send, pos_recv)
 
-    weights = []
-    for h in range(2):
-        wide[...] = jnp.zeros((128, 128), F32)
-        wide[:64, :64] = map_ref[2 * h]
-        wide[64:, 64:] = map_ref[2 * h + 1]
-        full = wide[...]
-        head = full.astype(BF16)
-        tail = (full - head.astype(F32)).astype(BF16)
-        line = jnp.concatenate([head, tail], axis=1)
-        weights.append(jnp.concatenate([line, line], axis=0))
-
+    weights = [weight_ref[0], weight_ref[1]]
     fetch(columns, 0, 0, block_ref)
     chunk = 512
 
@@ -228,34 +261,49 @@
 
     lax.fori_loop(0, view // chunk, mix_block, 0)
 
-    for copy in copies:
+    got = view + 16
+
+    def mix_got(first, last):
+        block_ref[got + first : got + last, :] = mix(recv[first:last, :], weights)
+
+    for copy in copies[4:]:
         copy.wait()
-    for k in range(4):
-        part = slice(k * 2 * NEAR, (k + 1) * 2 * NEAR)
-        got_ref[part, :] = mix(recv[part, :], weights)
-    part = slice(8 * NEAR, send.shape[0])
-    got_ref[part, :] = mix(recv[part, :], weights)
+    mix_got(8 * NEAR, send.shape[0])
+    for k in (2, 3, 0, 1):
+        copies[k].wait()
+        mix_got(k * 2 * NEAR, (k + 1) * 2 * NEAR)
     near_out[...] = near_in[...]
     far_out[...] = far_in[...]
 
 
-def place_kernel(near_ref, far_ref, block_in, got_ref, block_ref, out_ref, sem):
-    def put(count, source, index_ref, index):
+def place_kernel(near_ref, far_ref, block_in, block_ref, out_ref, sems):
+    view = out_ref.shape[0]
+    got = view + 16
+
+    def put(count, source, index_at):
         def body(i, carry):
-            rows = [got_ref[pl.ds(source + i * 16 + s, 2, stride=8), :] for s in range(8)]
+            rows = [block_ref[pl.ds(got + source + i * 16 + s, 2, stride=8), :] for s in range(8)]
             for s in range(8):
-                block_ref[pl.ds(index_ref[index + i * 8 + s], 2, stride=8), :] = rows[s]
+                block_ref[pl.ds(index_at(i * 8 + s), 2, stride=8), :] = rows[s]
             return carry
 
         lax.fori_loop(0, count // 8, body, 0)
 
     for k in range(4):
-        put(NEAR, k * 2 * NEAR, near_ref, k * NEAR_ROWS * 128)
-    for j in range(far_ref.shape[0] // 128):
-        put(8, 8 * NEAR + 16 * j, far_ref, j * 128)
-    copy = pltpu.make_async_copy(block_ref.at[pl.ds(0, out_ref.shape[0])], out_ref, sem)
-    copy.start()
-    copy.wait()
+        put(NEAR, k * 2 * NEAR, lambda i: near_ref[k * NEAR_ROWS * 128 + i])
+    for j in range(far_ref.shape[0]):
+        put(SPREAD, 8 * NEAR + 16 * j, lambda i: far_ref[j, 0, i])
+    piece = view // PIECES
+    stores = [
+        pltpu.make_async_copy(
+            block_ref.at[pl.ds(i * piece, piece)], out_ref.at[pl.ds(i * piece, piece)], sems.at[i]
+        )
+        for i in range(PIECES)
+    ]
+    for store in stores:
+        store.start()
+    for store in stores:
+        store.wait()
 
 
 def per_device(fields, file_offset, level_remap):
@@ -268,40 +316,46 @@
     total = -(-(rows + 4 * NEAR_ROWS + count) // 8) * 8
     vmem = pl.BlockSpec(memory_space=pltpu.VMEM)
     smem = pl.BlockSpec(memory_space=pltpu.SMEM)
-    hbm = pl.BlockSpec(memory_space=pl.ANY)
-
-    src, near_pos, far_pos = pl.pallas_call(
+    hbm = pl.BlockSpec(memory_space=pltpu.HBM)
+
+    view = fields.reshape(columns // 8, 8, 2, 128).transpose(0, 2, 1, 3).reshape(2 * columns, 128)
+    src, near_pos, far_pos, held, weights = pl.pallas_call(
         functools.partial(route_kernel, n_io, n_comp),
         out_shape=(
             jax.ShapeDtypeStruct((total, 128), I32),
             jax.ShapeDtypeStruct((4, NEAR_ROWS, 128), I32),
             jax.ShapeDtypeStruct((count, 1, 128), I32),
+            pltpu.VMEM((2 * columns, 128), F32),
+            pltpu.VMEM((2, 256, 256), BF16),
         ),
-        in_specs=[vmem],
-        out_specs=(vmem,) * 3,
+        in_specs=[hbm, hbm, hbm],
+        out_specs=(vmem,) * 5,
+        scratch_shapes=[
+            pltpu.VMEM(file_offset.shape, I32),
+            pltpu.VMEM(level_remap.shape, F32),
+            pltpu.VMEM((128, 128), F32),
+            pltpu.SemaphoreType.DMA((PIECES + 2,)),
+        ],
         compiler_params=pltpu.CompilerParams(vmem_limit_bytes=LIMIT),
         name="route",
-    )(file_offset)
-
-    view = fields.reshape(columns // 8, 8, 2, 128).transpose(0, 2, 1, 3).reshape(2 * columns, 128)
+    )(*[pltpu.with_memory_space_constraint(x, pltpu.HBM) for x in (file_offset, view, level_remap)])
+
     slots = 4 * NEAR + 8 * count
     kinds = 4 + count
-    block, got, near_got, far_got = pl.pallas_call(
+    block, near_got, far_got = pl.pallas_call(
         functools.partial(exchange_kernel, n_io, n_comp),
         out_shape=(
-            pltpu.VMEM((2 * columns + 16, 128), F32),
-            jax.ShapeDtypeStruct((2 * slots, 128), F32),
+            pltpu.VMEM((2 * columns + 16 + 2 * slots, 128), F32),
             jax.ShapeDtypeStruct((4, NEAR_ROWS, 128), I32),
             jax.ShapeDtypeStruct((count, 1, 128), I32),
         ),
         in_specs=[smem, vmem, vmem, vmem, vmem],
-        out_specs=(vmem,) * 4,
+        out_specs=(vmem,) * 3,
         scratch_shapes=[
             pltpu.VMEM((2 * slots, 128), F32),
             pltpu.VMEM((2 * slots, 128), F32),
             pltpu.VMEM((4, NEAR_ROWS, 128), I32),
             pltpu.VMEM((count, 1, 128), I32),
-            pltpu.VMEM((128, 128), F32),
             pltpu.SemaphoreType.DMA((kinds,)),
             pltpu.SemaphoreType.DMA((kinds,)),
             pltpu.SemaphoreType.DMA((kinds,)),
@@ -311,7 +365,7 @@
             collective_id=0, has_side_effects=True, vmem_limit_bytes=LIMIT
         ),
         name="exchange",
-    )(src.reshape(-1), near_pos, far_pos, view, level_remap)
+    )(src.reshape(-1), near_pos, far_pos, held, weights)
 
     _, out = pl.pallas_call(
         place_kernel,
@@ -319,13 +373,13 @@
             pltpu.VMEM(block.shape, F32),
             jax.ShapeDtypeStruct((2 * columns, 128), F32),
         ),
-        in_specs=[smem, smem, vmem, vmem],
+        in_specs=[smem, smem, vmem],
         out_specs=(vmem, hbm),
-        scratch_shapes=[pltpu.SemaphoreType.DMA],
+        scratch_shapes=[pltpu.SemaphoreType.DMA((PIECES,))],
         input_output_aliases={2: 0},
         compiler_params=pltpu.CompilerParams(vmem_limit_bytes=LIMIT),
         name="place",
-    )(near_got.reshape(-1), far_got.reshape(-1), block, got)
+    )(near_got.reshape(-1), far_got, block)
     return out.reshape(columns // 8, 2, 8, 128).transpose(0, 2, 1, 3).reshape(columns, width)
 
 

time: 28.6 us -> 25 us (0.87)
  local copies, waits for them, and re-layouts: 5.56 us -> 0 us
  Pallas kernels: 22.7 us -> 24.8 us
    unnamed x10 -> x0, local copies, waits for them, and re-layouts: 5.56 us -> none
    pallas_call x1, Pallas kernels: 0.99 us -> 2.03 us  [per_device(): pl.pallas_call(functools.partial(route_kernel, n_io, n_comp), out_shape=(...]
    pallas_call x1, Pallas kernels: 18.3 us -> 18.9 us  [per_device(): pl.pallas_call(functools.partial(exchange_kernel, n_io, n_comp), out_shap...]
    pallas_call x1, Pallas kernels: 3.48 us -> 3.88 us  [per_device(): pl.pallas_call(place_kernel, out_shape=(pltpu.VMEM(block.shape, F32), jax...]
where the time goes in v2:
time: 25 us; the launch traced here: 24.8 us
  Pallas kernels  24.8 us (99%)
    pallas_call x1, Pallas kernels, per_device(): pl.pallas_call(functools.partial(exchange_kernel, n_io, n_comp), out_shap...  18.9 us
    pallas_call x1, Pallas kernels, per_device(): pl.pallas_call(place_kernel, out_shape=(pltpu.VMEM(block.shape, F32), jax...  3.88 us
    pallas_call x1, Pallas kernels, per_device(): pl.pallas_call(functools.partial(route_kernel, n_io, n_comp), out_shape=(...  2.03 us

profile of v2, /device:TPU:0, one launch (start us, length us, event | category | flops | bytes accessed | tf_op | source)
XLA Modules:
  0.0 24.8 jit_solution(10415112966659234180)
XLA Ops:
  0.0 2.0 %route.1 = (s32[40,128]{1,0:T(8,128)S(1)}, s32[4,2,128]{2,1,0:T(2,128)S(1)}, s32[6,1,128]{2,1,0:T(1,128)S(1)}, f32[6144,128]{1,0:T(8,128)S(1)}, bf16[2,256,256]{2,1,0:T(8,128)(2,1)S(1)}) custom-call(s32[24,128]{1,0:T(8,128)} %off_hbm.1, f32[6144,128]{1,0:T(8,128)} %bitcast.14, f32[4,64,64]{2,1,0:T(8,128)} %map_hbm.1), custom_call_target="tpu_custom_call" | custom-call | tf_op jit(solution)/shard_map/route/pallas_call | solution.py:322
  2.0 18.9 %exchange.1 = (f32[7856,128]{1,0:T(8,128)S(1)}, s32[4,2,128]{2,1,0:T(2,128)S(1)}, s32[6,1,128]{2,1,0:T(1,128)S(1)}) custom-call(s32[5120]{0:T(1024)S(1)} %bitcast.12, s32[4,2,128]{2,1,0:T(2,128)S(1)} %get-tuple-element.15.near_ref, s32[6,1,128]{2,1,0:T(1,128)S(1)} %get-tuple-element.16.far_ref, f32[6144,128]{1,0:T(8,128)S(1)} %get-tuple-element.17.fields_ref, ...), custom_call_target="tpu_custom_call" | custom-call | tf_op jit(solution)/shard_map/exchange/pallas_call | solution.py:345
  21.0 3.9 %place.1 = (f32[7856,128]{1,0:T(8,128)S(1)}, f32[6144,128]{1,0:T(8,128)}) custom-call(s32[1024]{0:T(1024)S(1)} %bitcast.13, s32[6,1,128]{2,1,0:T(1,128)S(1)} %get-tuple-element.20.far_ref, f32[7856,128]{1,0:T(8,128)S(1)} %get-tuple-element.21.block_in), custom_call_target="tpu_custom_call", output_to_operand_aliasing={{0}: (2, {})} | custom-call | tf_op jit(solution)/shard_map/place/pallas_call | solution.py:370

commit v3 on v2

--- a/solution.py
+++ b/solution.py
@@ -209,17 +209,19 @@
         )
 
     def fetch(count, source, target, target_ref):
+        lines = 5 if count % 40 == 0 else 4 if count % 32 == 0 else 1
+
         def body(i, carry):
-            got = [
-                fields_ref[pl.ds(src_ref[source + i * 8 + s], 2, stride=8), :] for s in range(8)
-            ]
-            for s in range(8):
-                target_ref[pl.ds(target + i * 16 + s, 2, stride=8), :] = got[s]
+            got = []
+            for s in range(8 * lines):
+                at = source + i * 8 * lines + s
+                got.append(fields_ref[pl.ds(src_ref[at], 2, stride=8), :])
+            for s in range(8 * lines):
+                to = target + i * 16 * lines + 16 * (s // 8) + s % 8
+                target_ref[pl.ds(to, 2, stride=8), :] = got[s]
             return carry
 
-        lax.fori_loop(0, count // 8, body, 0)
-
-    copies = []
+        lax.fori_loop(0, count // (8 * lines), body, 0)
 
     def ship(source, target, sem_at, axis, step, sends, recvs):
         copy = pltpu.make_async_remote_copy(
@@ -231,24 +233,27 @@
             device_id_type=pl.DeviceIdType.MESH,
         )
         copy.start()
-        copies.append(copy)
-
-    for k in range(4):
+        return copy
+
+    def ship_near(k):
         fetch(NEAR, columns + k * NEAR_ROWS * 128, k * 2 * NEAR, send)
         if k == 0:
             pl.semaphore_wait(barrier, len(everyone))
         axis, step = near[k]
         part = pl.ds(k * 2 * NEAR, 2 * NEAR)
-        ship(send.at[part], recv.at[part], k, axis, step, row_send, row_recv)
+        return ship(send.at[part], recv.at[part], k, axis, step, row_send, row_recv)
+
+    near_copies = [ship_near(0), ship_near(1)]
+    small = []
+    for k, (axis, step) in enumerate(near):
+        small.append(ship(near_ref.at[k], near_in.at[k], k, axis, step, pos_send, pos_recv))
     for j, (axis, step) in enumerate(far):
+        small.append(ship(far_ref.at[j], far_in.at[j], 4 + j, axis, step, pos_send, pos_recv))
         start = 8 * NEAR + 16 * j
         fetch(8, columns + (4 * NEAR_ROWS + j) * 128, start, send)
         part = pl.ds(start, 16)
-        ship(send.at[part], recv.at[part], 4 + j, axis, step, row_send, row_recv)
-    for k, (axis, step) in enumerate(near):
-        ship(near_ref.at[k], near_in.at[k], k, axis, step, pos_send, pos_recv)
-    for j, (axis, step) in enumerate(far):
-        ship(far_ref.at[j], far_in.at[j], 4 + j, axis, step, pos_send, pos_recv)
+        small.append(ship(send.at[part], recv.at[part], 4 + j, axis, step, row_send, row_recv))
+    near_copies += [ship_near(2), ship_near(3)]
 
     weights = [weight_ref[0], weight_ref[1]]
     fetch(columns, 0, 0, block_ref)
@@ -266,11 +271,11 @@
     def mix_got(first, last):
         block_ref[got + first : got + last, :] = mix(recv[first:last, :], weights)
 
-    for copy in copies[4:]:
+    for copy in small:
         copy.wait()
     mix_got(8 * NEAR, send.shape[0])
     for k in (2, 3, 0, 1):
-        copies[k].wait()
+        near_copies[k].wait()
         mix_got(k * 2 * NEAR, (k + 1) * 2 * NEAR)
     near_out[...] = near_in[...]
     far_out[...] = far_in[...]
@@ -281,13 +286,17 @@
     got = view + 16
 
     def put(count, source, index_at):
+        lines = 5 if count % 40 == 0 else 1
+
         def body(i, carry):
-            rows = [block_ref[pl.ds(got + source + i * 16 + s, 2, stride=8), :] for s in range(8)]
-            for s in range(8):
-                block_ref[pl.ds(index_at(i * 8 + s), 2, stride=8), :] = rows[s]
+            for t in range(lines):
+                at = i * lines + t
+                rows = [block_ref[pl.ds(got + source + at * 16 + s, 2, stride=8), :] for s in range(8)]
+                for s in range(8):
+                    block_ref[pl.ds(index_at(at * 8 + s), 2, stride=8), :] = rows[s]
             return carry
 
-        lax.fori_loop(0, count // 8, body, 0)
+        lax.fori_loop(0, count // (8 * lines), body, 0)
 
     for k in range(4):
         put(NEAR, k * 2 * NEAR, lambda i: near_ref[k * NEAR_ROWS * 128 + i])

time: 25 us -> 24.4 us (0.976)
  Pallas kernels: 24.8 us -> 24.2 us
    pallas_call x1, Pallas kernels: 3.88 us -> 3.37 us  [per_device(): pl.pallas_call(place_kernel, out_shape=(pltpu.VMEM(block.shape, F32), jax...]
where the time goes in v3:
time: 24.4 us; the launch traced here: 24.2 us
  Pallas kernels  24.2 us (99%)
    pallas_call x1, Pallas kernels, per_device(): pl.pallas_call(functools.partial(exchange_kernel, n_io, n_comp), out_shap...  18.8 us
    pallas_call x1, Pallas kernels, per_device(): pl.pallas_call(place_kernel, out_shape=(pltpu.VMEM(block.shape, F32), jax...  3.37 us
    pallas_call x1, Pallas kernels, per_device(): pl.pallas_call(functools.partial(route_kernel, n_io, n_comp), out_shape=(...  2.03 us

profile of v3, /device:TPU:0, one launch (start us, length us, event | category | flops | bytes accessed | tf_op | source)
XLA Modules:
  0.0 24.2 jit_solution(1479864093975764806)
XLA Ops:
  0.0 2.0 %route.1 = (s32[40,128]{1,0:T(8,128)S(1)}, s32[4,2,128]{2,1,0:T(2,128)S(1)}, s32[6,1,128]{2,1,0:T(1,128)S(1)}, f32[6144,128]{1,0:T(8,128)S(1)}, bf16[2,256,256]{2,1,0:T(8,128)(2,1)S(1)}) custom-call(s32[24,128]{1,0:T(8,128)} %off_hbm.1, f32[6144,128]{1,0:T(8,128)} %bitcast.14, f32[4,64,64]{2,1,0:T(8,128)} %map_hbm.1), custom_call_target="tpu_custom_call" | custom-call | tf_op jit(solution)/shard_map/route/pallas_call | solution.py:331
  2.0 18.8 %exchange.1 = (f32[7856,128]{1,0:T(8,128)S(1)}, s32[4,2,128]{2,1,0:T(2,128)S(1)}, s32[6,1,128]{2,1,0:T(1,128)S(1)}) custom-call(s32[5120]{0:T(1024)S(1)} %bitcast.12, s32[4,2,128]{2,1,0:T(2,128)S(1)} %get-tuple-element.15.near_ref, s32[6,1,128]{2,1,0:T(1,128)S(1)} %get-tuple-element.16.far_ref, f32[6144,128]{1,0:T(8,128)S(1)} %get-tuple-element.17.fields_ref, ...), custom_call_target="tpu_custom_call" | custom-call | tf_op jit(solution)/shard_map/exchange/pallas_call | solution.py:354
  20.8 3.4 %place.1 = (f32[7856,128]{1,0:T(8,128)S(1)}, f32[6144,128]{1,0:T(8,128)}) custom-call(s32[1024]{0:T(1024)S(1)} %bitcast.13, s32[6,1,128]{2,1,0:T(1,128)S(1)} %get-tuple-element.20.far_ref, f32[7856,128]{1,0:T(8,128)S(1)} %get-tuple-element.21.block_in), custom_call_target="tpu_custom_call", output_to_operand_aliasing={{0}: (2, {})} | custom-call | tf_op jit(solution)/shard_map/place/pallas_call | solution.py:379
